TPU v7x, 32 devices: a whole 2x2x4 slice. The times are simulated.
32 devices in a mesh: cfg: 2 (over y), seq: 8 (over z, core), tp: 2 (over x).
Axes of the slice: x: 2, y: 2, z: 4, core: 2. Of those that a mesh axis runs over, the one named last changes fastest.
Arguments:
- queries: bfloat16 [2, 3840, 5120], P('cfg', 'seq', 'tp'), may hold values from -5 to 5
- keys: bfloat16 [2, 3840, 5120], P('cfg', 'seq', 'tp'), may hold values from -5 to 5
- values: bfloat16 [2, 3840, 5120], P('cfg', 'seq', 'tp'), may hold values from -5 to 5
- text_keys: bfloat16 [2, 512, 5120], P('cfg', None, 'tp'), may hold values from -7.5 to 7.5
- text_values: bfloat16 [2, 512, 5120], P('cfg', None, 'tp'), may hold values from -5 to 5
- prompt_lengths: int32 [2], P('cfg'), may hold values from 64 to 512
- frame_counts: int32 [8], P('seq'), may hold values from 240 to 480
- out_weight: bfloat16 [5120, 5120], P('tp'), may hold values from -0.5 to 0.5
Outputs:
- velocity: bfloat16 [3840, 5120], P('seq', ('tp', 'cfg'))
All inputs are finite; a program needn't handle non-finite values.
Results may differ from a plain program's by a relative error of at most 0.015.
Values may be sent and summed in bfloat16 or wider, within the bound.
A program may use at most 320 MiB of HBM per device.

v0:
```python
import jax
import jax.numpy as jnp
from jax import lax
from jax.sharding import PartitionSpec as P

HEAD_DIM = 128
FRAME_SLOTS = 480
GUIDANCE = 5.0
RESCALE = 0.7
NEGATIVE = -1e30


def frame_valid(positions, counts_table):
    frame_index = positions // FRAME_SLOTS
    slot_index = positions % FRAME_SLOTS
    frame_ids = jnp.arange(counts_table.shape[0], dtype=jnp.int32)
    frame_limit = jnp.sum(
        jnp.where(frame_index[:, None] == frame_ids[None, :], counts_table[None, :], 0), axis=1
    )
    return slot_index < frame_limit


def attend_block(carry, key_rows, value_rows, query_heads, key_mask):
    row_max, weight_sum, mixed_sum = carry
    head_count = query_heads.shape[1]
    key_heads = key_rows.reshape(key_rows.shape[0], head_count, HEAD_DIM)
    value_heads = value_rows.reshape(value_rows.shape[0], head_count, HEAD_DIM)
    scores = jnp.einsum(
        "qhd,khd->hqk", query_heads, key_heads, preferred_element_type=jnp.float32
    ) * HEAD_DIM ** (-0.5)
    scores = jnp.where(key_mask[None, None, :], scores, NEGATIVE)
    new_max = jnp.maximum(row_max, jnp.max(scores, axis=2))
    shrink = jnp.exp(row_max - new_max)
    weights = jnp.exp(scores - new_max[:, :, None])
    weight_sum = weight_sum * shrink + jnp.sum(weights, axis=2)
    mixed_sum = mixed_sum * shrink[:, :, None] + jnp.einsum(
        "hqk,khd->hqd",
        weights.astype(jnp.bfloat16),
        value_heads,
        preferred_element_type=jnp.float32,
    )
    return (new_max, weight_sum, mixed_sum)


def body(queries, keys, values, text_keys, text_values, prompt_lengths, frame_counts, out_weight):
    row_count = queries.shape[1]
    head_cols = queries.shape[2]
    head_count = head_cols // HEAD_DIM
    all_counts = lax.all_gather(frame_counts, "seq", axis=0, tiled=True)
    query_heads = queries[0].reshape(row_count, head_count, HEAD_DIM)
    text_mask = jnp.arange(text_keys.shape[1], dtype=jnp.int32) < prompt_lengths[0]
    empty_state = (
        jnp.full((head_count, row_count), NEGATIVE, jnp.float32),
        jnp.zeros((head_count, row_count), jnp.float32),
        jnp.zeros((head_count, row_count, HEAD_DIM), jnp.float32),
    )
    text_state = attend_block(empty_state, text_keys[0], text_values[0], query_heads, text_mask)
    key_rows = lax.all_gather(keys[0], "seq", axis=0, tiled=True)
    value_rows = lax.all_gather(values[0], "seq", axis=0, tiled=True)
    positions = jnp.arange(key_rows.shape[0], dtype=jnp.int32)
    row_max, weight_sum, mixed_sum = attend_block(
        text_state, key_rows, value_rows, query_heads, frame_valid(positions, all_counts)
    )
    attended = (
        jnp.transpose(mixed_sum / weight_sum[:, :, None], (1, 0, 2))
        .reshape(row_count, head_cols)
        .astype(jnp.bfloat16)
    )
    projected = (
        lax.psum_scatter(
            lax.dot_general(
                out_weight, attended, (((0,), (1,)), ((), ())), preferred_element_type=jnp.float32
            ).astype(jnp.bfloat16),
            "tp",
            scatter_dimension=0,
            tiled=True,
        )
        .astype(jnp.float32)
        .T
    )
    branch = projected.astype(jnp.bfloat16)[None]
    half_cols = head_cols // 2
    gathered = lax.all_gather(branch, "cfg", axis=0, tiled=True)
    paired = lax.dynamic_slice_in_dim(gathered, lax.axis_index("cfg") * half_cols, half_cols, 2)
    conditional = paired[0].astype(jnp.float32)
    unconditional = paired[1].astype(jnp.float32)
    guided = unconditional + GUIDANCE * (conditional - unconditional)
    token_weights = frame_valid(jnp.arange(row_count, dtype=jnp.int32), frame_counts).astype(
        jnp.float32
    )

    def local_sum(field_rows):
        return jnp.dot(token_weights, field_rows, precision=lax.Precision.HIGHEST)

    guided_sum, guided_square, cond_sum, cond_square = lax.psum(
        (
            local_sum(guided),
            local_sum(guided * guided),
            local_sum(conditional),
            local_sum(conditional * conditional),
        ),
        "seq",
    )
    valid_total = jnp.sum(all_counts).astype(jnp.float32)
    guided_mean = guided_sum / valid_total
    guided_var = guided_square / valid_total - guided_mean * guided_mean
    cond_mean = cond_sum / valid_total
    cond_var = cond_square / valid_total - cond_mean * cond_mean
    std_ratio = jnp.sqrt((cond_var + 1.0) / (guided_var + 1.0))
    factor = RESCALE * std_ratio + (1.0 - RESCALE)
    return (guided_mean + (guided - guided_mean) * factor).astype(jnp.bfloat16)


def solution(mesh):
    placed = (
        P("cfg", "seq", "tp"),
        P("cfg", "seq", "tp"),
        P("cfg", "seq", "tp"),
        P("cfg", None, "tp"),
        P("cfg", None, "tp"),
        P("cfg"),
        P("seq"),
        P("tp", None),
    )
    return jax.shard_map(
        body, mesh=mesh, in_specs=placed, out_specs=P("seq", ("tp", "cfg")), check_vma=False
    )
```

profile of v0, /device:TPU:0, one launch (start us, length us, event | category | flops | bytes accessed | tf_op | source)
XLA Modules:
  0.0 636.8 jit_solution(17651519796824386608)
XLA Ops:
  6.5 0.0 copy-start.4
  6.5 0.0 all-gather.7.cloned.1.call-start
  6.5 0.7 all-gather.7.cloned.1.call-update
  7.3 0.0 all-gather.9.cloned.1.call-start
  7.3 0.7 all-gather.9.cloned.1.call-update
  8.0 0.0 reduce-scatter.2.cloned.1.call-start
  8.7 0.0 copy-done.4
  8.7 0.6 dynamic-slice
  9.3 0.7 dynamic-update-slice
  10.0 10.6 %all-reduce = s32[8]{0:T(128)S(1)} all-reduce(s32[8]{0:T(128)S(1)} %dynamic-update-slice), channel_id=1, replica_groups=mesh['cfg'=2,'seq'=8,'tp'=2] {'seq'}, use_global_device_ids=true, to_apply=%add | all-reduce | flops 8 | bytes 64
  20.6 0.0 copy-start.2
  20.6 3.2 copy.37
  24.4 4.5 copy.38
  28.9 4.4 copy.41
  33.4 0.0 copy-done.2
  33.4 0.1 select_reduce_fusion
  33.5 12.2 %fusion.6 = (f32[20,480]{1,0:T(8,128)S(1)}, f32[20,480,512]{2,1,0:T(8,128)}) fusion(pred[512]{0:T(512)(128)(4,1)S(1)} %iota_compare_fusion.2, bf16[480,20,128]{0,2,1:T(8,128)(2,1)S(1)} %bitcast.86, bf16[512,20,128]{0,2,1:T(8,128)(2,1)} %bitcast.89), kind=kOutput, calls=%fused_computation.9 | convolution fusion | flops 1273027200 | bytes 24778752 | tf_op jit(solution)/shard_map/qhd,khd->hqk/dot_general | solution.py:28
  45.7 140.8 %all-gather.7.cloned.1.call-done = bf16[1,3840,2560]{2,1,0:T(8,128)(2,1)} async-done(((bf16[1,480,2560]{2,1,0:T(8,128)(2,1)}), bf16[1,3840,2560]{2,1,0:T(8,128)(2,1)}) %all-gather.7.cloned.1.call-update) | async-done | bytes 19660816 | tf_op jit(solution)/shard_map/all_gather | solution.py:58
  186.5 25.5 %copy.43 = bf16[1,3840,2560]{1,2,0:T(8,128)(2,1)} copy(bf16[1,3840,2560]{2,1,0:T(8,128)(2,1)} %all-gather.7.cloned.1.call-done) | data formatting | bytes 39321600 | tf_op jit(solution)/shard_map/all_gather | solution.py:58
  211.9 58.6 %fusion = (f32[20,480]{1,0:T(8,128)S(1)}, f32[20,480,3840]{2,1,0:T(8,128)}) fusion(pred[3840]{0:T(1024)(128)(4,1)S(1)} %fusion.37, bf16[480,20,128]{0,2,1:T(8,128)(2,1)S(1)} %bitcast.87, bf16[3840,20,128]{0,2,1:T(8,128)(2,1)} %bitcast.85), kind=kOutput, calls=%fused_computation.2 | convolution fusion | flops 9547766784 | bytes 169616640 | tf_op jit(solution)/shard_map/qhd,khd->hqk/dot_general | solution.py:28
  270.5 9.7 %fusion.7 = f32[20,480]{1,0:T(8,128)S(1)} fusion(f32[20,480,512]{2,1,0:T(8,128)} %get-tuple-element.19, f32[20,480]{1,0:T(8,128)S(1)} %get-tuple-element.13, pred[512]{0:T(512)(128)(4,1)S(1)} %iota_compare_fusion.2), kind=kLoop, calls=%fused_computation.10 | loop fusion | flops 19651200 | bytes 19738112 | tf_op jit(solution)/shard_map/reduce_sum | solution.py:35
  280.2 0.0 copy-start.1
  280.2 45.5 %fusion.1 = f32[20,480]{1,0:T(8,128)S(1)} fusion(f32[20,480,3840]{2,1,0:T(8,128)} %get-tuple-element.17, f32[20,480]{1,0:T(8,128)S(1)} %get-tuple-element.12, pred[3840]{0:T(1024)(128)(4,1)S(1)} %fusion.37), kind=kLoop, calls=%fused_computation.3 | loop fusion | flops 147446400 | bytes 147536640 | tf_op jit(solution)/shard_map/reduce_sum | solution.py:35
  325.8 0.0 copy-done.1
  325.8 10.5 %fusion.9 = f32[20,480,128]{2,1,0:T(8,128)} fusion(bf16[512,20,128]{0,2,1:T(8,128)(2,1)S(1)} %bitcast.95, f32[20,480,512]{2,1,0:T(8,128)} %get-tuple-element.19, f32[20,480]{1,0:T(8,128)S(1)} %get-tuple-element.13, pred[512]{0:T(512)(128)(4,1)S(1)} %iota_compare_fusion.2), kind=kOutput, calls=%fused_computation.12 | convolution fusion | flops 1277952000 | bytes 27236352 | tf_op jit(solution)/shard_map/hqk,khd->hqd/dot_general | solution.py:36
  336.2 24.8 %all-gather.9.cloned.1.call-done = bf16[1,3840,2560]{2,1,0:T(8,128)(2,1)} async-done(((bf16[1,480,2560]{2,1,0:T(8,128)(2,1)}), bf16[1,3840,2560]{2,1,0:T(8,128)(2,1)}) %all-gather.9.cloned.1.call-update) | async-done | bytes 19660816 | tf_op jit(solution)/shard_map/all_gather | solution.py:59
  361.0 24.1 %copy.46 = bf16[1,3840,2560]{1,2,0:T(8,128)(2,1)} copy(bf16[1,3840,2560]{2,1,0:T(8,128)(2,1)} %all-gather.9.cloned.1.call-done) | data formatting | bytes 39321600 | tf_op jit(solution)/shard_map/all_gather | solution.py:59
  385.1 55.6 %fusion.17 = bf16[480,20,128]{2,0,1:T(8,128)(2,1)} fusion(f32[20,480,128]{2,1,0:T(8,128)} %fusion.9, f32[480,20]{0,1:T(8,128)S(1)} %get-tuple-element.9, f32[480,20]{0,1:T(8,128)S(1)} %get-tuple-element.10, f32[480,20]{0,1:T(8,128)S(1)} %get-tuple-element.11, bf16[3840,20,128]{0,2,1:T(8,128)(2,1)} %bitcast.88, f32[20,480,3840]{2,1,0:T(8,128)} %get-tuple-element.17, ...), kind=kOutput, calls=%fused_computation.21 | convolution fusion | flops 9590784000 | bytes 174647040 | tf_op jit(solution)/shard_map/hqk,khd->hqd/dot_general | solution.py:36
  440.7 2.9 copy.48
  443.6 19.5 %fusion.15 = bf16[5120,480]{0,1:T(8,128)(2,1)} fusion(bf16[480,2560]{0,1:T(8,128)(2,1)S(1)} %bitcast.96, bf16[2560,5120]{1,0:T(8,128)(2,1)} %param.15), kind=kOutput, calls=%fused_computation.18 | convolution fusion | flops 12585369600 | bytes 33587200 | tf_op jit(solution)/shard_map/dot_general | solution.py:71
  463.2 0.0 copy-start.3
  463.2 0.0 reduce-scatter.2.cloned.1.call-update
  463.2 0.0 all-gather.11.cloned.1.call-start
  463.2 60.5 %reduce-scatter.2.cloned.1.call-done = bf16[2560,480]{0,1:T(8,128)(2,1)} async-done(((bf16[5120,480]{0,1:T(8,128)(2,1)}), bf16[2560,480]{0,1:T(8,128)(2,1)}) %reduce-scatter.2.cloned.1.call-update) | async-done | bytes 2457616 | tf_op jit(solution)/shard_map/reduce_scatter | solution.py:70
  523.7 0.0 all-gather.11.cloned.1.call-update
  523.7 0.0 copy-done.3
  523.8 0.7 reduce_sum.49
  525.1 65.0 %all-gather.11.cloned.1.call-done = bf16[960,2560]{1,0:T(8,128)(2,1)} async-done(((bf16[480,2560]{1,0:T(8,128)(2,1)}), bf16[960,2560]{1,0:T(8,128)(2,1)}) %all-gather.11.cloned.1.call-update) | async-done | bytes 4915216 | tf_op jit(solution)/shard_map/all_gather | solution.py:83
  590.0 0.0 copy-start
  590.0 1.7 convolution_reduce_fusion
  591.7 2.4 fusion.28
  594.2 2.9 fusion.29
  597.1 0.0 copy-done
  597.2 1.4 fusion.30
  598.5 28.4 %all-reduce.1 = (f32[1280]{0:T(1024)S(1)}, f32[1280]{0:T(1024)S(1)}, f32[1280]{0:T(1024)S(1)}, f32[1280]{0:T(1024)S(1)}) all-reduce(f32[1280]{0:T(1024)S(1)} %fusion.30, f32[1280]{0:T(1024)S(1)} %convolution_reduce_fusion, f32[1280]{0:T(1024)S(1)} %fusion.28, f32[1280]{0:T(1024)S(1)} %fusion.29), channel_id=1, replica_groups=mesh['cfg'=2,'seq'=8,'tp'=2] {'seq'}, use_global_device_ids=true, to_apply=%region_10.11 | all-reduce | flops 5120 | bytes 40960 | tf_op jit(solution)/shard_map/psum | solution.py:95
  626.9 3.4 add_convert_fusion
  (9 shorter events, 0.1 us)
Async XLA Ops:
  6.5 2.2 copy-start.4
  6.5 179.9 %all-gather.7.cloned.1.call-start = ((), (), s32[]{:S(2)}) async-start(), calls=%async_computation.2 | async-start | bytes 22118400 | tf_op jit(solution)/shard_map/all_gather | solution.py:58
  7.3 353.8 %all-gather.9.cloned.1.call-start = ((), (), s32[]{:S(2)}) async-start(), calls=%async_computation.3 | async-start | bytes 22118400 | tf_op jit(solution)/shard_map/all_gather | solution.py:59
  8.0 515.7 %reduce-scatter.2.cloned.1.call-start = ((), (), s32[]{:S(2)}) async-start(), calls=%async_computation.1 | async-start | bytes 7372800 | tf_op jit(solution)/shard_map/reduce_scatter | solution.py:70
  20.6 12.8 %copy-start.2 = (s32[8]{0:T(128)}, s32[8]{0:T(128)S(1)}, u32[]{:S(2)}) copy-start(s32[8]{0:T(128)S(1)} %all-reduce) | copy-start | bytes 100
  280.2 45.6 %copy-start.1 = (bf16[1,512,2560]{1,2,0:T(8,128)(2,1)S(1)}, bf16[1,512,2560]{1,2,0:T(8,128)(2,1)}, u32[]{:S(2)}) copy-start(bf16[1,512,2560]{1,2,0:T(8,128)(2,1)} %copy.41) | copy-start | bytes 7864324
  463.2 60.6 %copy-start.3 = (s32[8]{0:T(128)S(1)}, s32[8]{0:T(128)}, u32[]{:S(2)}) copy-start(s32[8]{0:T(128)} %copy-done.2) | copy-start | bytes 100
  463.2 126.8 %all-gather.11.cloned.1.call-start = ((), (), s32[]{:S(2)}) async-start(), calls=%async_computation.4 | async-start | bytes 7372800 | tf_op jit(solution)/shard_map/all_gather | solution.py:83
  590.0 7.1 %copy-start = (bf16[960,2560]{1,0:T(8,128)(2,1)S(1)}, bf16[960,2560]{1,0:T(8,128)(2,1)}, u32[]{:S(2)}) copy-start(bf16[960,2560]{1,0:T(8,128)(2,1)} %all-gather.11.cloned.1.call-done) | copy-start | bytes 14745604
Sparse Core Ops, SparseCore 0:
  9.0 177.4 all-gather.6
  188.1 172.8 all-gather.8
  463.3 60.3 reduce-scatter.1
  525.1 64.8 all-gather.10
where the time goes:
time: 639 us; the launch traced here: 637 us
  waiting for transfers between devices  292 us (46%)
  matrix products  165 us (26%)
  local copies, waits for them, and re-layouts  65.8 us (10%)
  other arithmetic  59.5 us (9%)
  blocking collectives  39 us (6%)
  between operations  15.2 us (2%)
    all_gather x1, waiting for transfers between devices, body(): key_rows = lax.all_gather(keys[0], 'seq', axis=0, tiled=True)  141 us
    dot_general x2, matrix products, attend_block(): jnp.einsum('qhd,khd->hqk', query_heads, key_heads, preferred_element_type...  70.7 us
    dot_general x2, matrix products, attend_block(): jnp.einsum('hqk,khd->hqd', weights.astype(jnp.bfloat16), value_heads, pre...  66.1 us
    all_gather x1, waiting for transfers between devices, body(): gathered = lax.all_gather(branch, 'cfg', axis=0, tiled=True)  65 us
    reduce_scatter x1, waiting for transfers between devices, body(): lax.psum_scatter(lax.dot_general(out_weight, attended, (((0,), (1,)), (()...  60.5 us
    reduce_sum x2, other arithmetic, attend_block(): weight_sum = weight_sum * shrink + jnp.sum(weights, axis=2)  55.2 us
    psum x1, blocking collectives, body(): lax.psum((local_sum(guided), local_sum(guided * guided), local_sum(condit...  28.4 us
    all_gather x1, local copies, waits for them, and re-layouts, body(): key_rows = lax.all_gather(keys[0], 'seq', axis=0, tiled=True)  25.5 us
  transfers between devices with their start and end apart: 4, of which 4 were waited for; matrix products, arithmetic and copies ran while one was open for 28% of the time, Pallas kernels for 0%

commit v1 on v0

--- a/solution.py
+++ b/solution.py
@@ -55,7 +55,12 @@
         jnp.zeros((head_count, row_count, HEAD_DIM), jnp.float32),
     )
     text_state = attend_block(empty_state, text_keys[0], text_values[0], query_heads, text_mask)
-    key_rows = lax.all_gather(keys[0], "seq", axis=0, tiled=True)
+    ring = [keys[0]]
+    for hop in range(7):
+        ring.append(lax.ppermute(ring[-1], "seq", [(dev, (dev + 1) % 8) for dev in range(8)]))
+    key_rows = jnp.roll(
+        jnp.concatenate(ring[::-1], axis=0), (lax.axis_index("seq") + 1) * ring[0].shape[0], axis=0
+    )
     value_rows = lax.all_gather(values[0], "seq", axis=0, tiled=True)
     positions = jnp.arange(key_rows.shape[0], dtype=jnp.int32)
     row_max, weight_sum, mixed_sum = attend_block(

time: 639 us -> 924 us (1.45)
  waiting for transfers between devices: 292 us -> 475 us
  local copies, waits for them, and re-layouts: 65.8 us -> 160 us
    ppermute x0 -> x7, waiting for transfers between devices: none -> 328 us  [body(): lax.ppermute(ring[-1], 'seq', [(dev, (dev + 1) % 8) for dev in range(8)])]
    all_gather x1 -> x0, waiting for transfers between devices: 141 us -> none  [body(): key_rows = lax.all_gather(keys[0], 'seq', axis=0, tiled=True)]
    concatenate x0 -> x1, local copies, waits for them, and re-layouts: none -> 60.8 us  [body(): jnp.roll(jnp.concatenate(ring[::-1], axis=0), (lax.axis_index('seq') + 1)...]
    ppermute x0 -> x7, local copies, waits for them, and re-layouts: none -> 30.6 us  [body(): lax.ppermute(ring[-1], 'seq', [(dev, (dev + 1) % 8) for dev in range(8)])]
    all_gather x1 -> x0, local copies, waits for them, and re-layouts: 25.5 us -> none  [body(): key_rows = lax.all_gather(keys[0], 'seq', axis=0, tiled=True)]
    all_gather x1, waiting for transfers between devices: 24.8 us -> 0.01 us  [body(): value_rows = lax.all_gather(values[0], 'seq', axis=0, tiled=True)]
    reduce_scatter x1, waiting for transfers between devices: 60.5 us -> 81.9 us  [body(): lax.psum_scatter(lax.dot_general(out_weight, attended, (((0,), (1,)), (()...]
    dynamic_slice x0 -> x1, local copies, waits for them, and re-layouts: none -> 19.2 us  [body(): jnp.roll(jnp.concatenate(ring[::-1], axis=0), (lax.axis_index('seq') + 1)...]
  transfers between devices with their start and end apart: 4 -> 10, of which waited for: 4 -> 8; matrix products, arithmetic and copies ran while one was open for 28% -> 29% of each run, Pallas kernels for 0% -> 0%
where the time goes in v1:
time: 924 us; the launch traced here: 916 us
  waiting for transfers between devices  475 us (51%)
  matrix products  163 us (18%)
  local copies, waits for them, and re-layouts  160 us (17%)
  other arithmetic  59 us (6%)
  blocking collectives  41.9 us (5%)
  between operations  15.2 us (2%)
    ppermute x7, waiting for transfers between devices, body(): lax.ppermute(ring[-1], 'seq', [(dev, (dev + 1) % 8) for dev in range(8)])  328 us
    reduce_scatter x1, waiting for transfers between devices, body(): lax.psum_scatter(lax.dot_general(out_weight, attended, (((0,), (1,)), (()...  81.9 us
    dot_general x2, matrix products, attend_block(): jnp.einsum('qhd,khd->hqk', query_heads, key_heads, preferred_element_type...  69.2 us
    dot_general x2, matrix products, attend_block(): jnp.einsum('hqk,khd->hqd', weights.astype(jnp.bfloat16), value_heads, pre...  65.9 us
    all_gather x1, waiting for transfers between devices, body(): gathered = lax.all_gather(branch, 'cfg', axis=0, tiled=True)  65.1 us
    concatenate x1, local copies, waits for them, and re-layouts, body(): jnp.roll(jnp.concatenate(ring[::-1], axis=0), (lax.axis_index('seq') + 1)...  60.8 us
    reduce_sum x2, other arithmetic, attend_block(): weight_sum = weight_sum * shrink + jnp.sum(weights, axis=2)  54.7 us
    ppermute x7, local copies, waits for them, and re-layouts, body(): lax.ppermute(ring[-1], 'seq', [(dev, (dev + 1) % 8) for dev in range(8)])  30.6 us
  transfers between devices with their start and end apart: 10, of which 8 were waited for; matrix products, arithmetic and copies ran while one was open for 29% of the time, Pallas kernels for 0%

profile of v1, /device:TPU:0, one launch (start us, length us, event | category | flops | bytes accessed | tf_op | source)
XLA Modules:
  0.0 915.6 jit_solution(1224017717339372455)
XLA Ops:
  6.5 0.5 collective-permute-start
  7.0 31.8 %collective-permute-done = bf16[480,2560]{1,0:T(8,128)(2,1)S(1)} collective-permute-done((bf16[480,2560]{1,0:T(8,128)(2,1)}, bf16[480,2560]{1,0:T(8,128)(2,1)S(1)}, u32[]{:S(2)}, u32[]{:S(2)}) %collective-permute-start) | collective-permute-done | bytes 2457632 | tf_op jit(solution)/shard_map/ppermute | solution.py:60
  38.8 0.0 all-gather.5.cloned.1.call-update
  38.9 0.0 reduce-scatter.2.cloned.1.call-start
  38.9 60.8 %collective-permute-done.1 = bf16[480,2560]{1,0:T(8,128)(2,1)} collective-permute-done((bf16[480,2560]{1,0:T(8,128)(2,1)S(1)}, bf16[480,2560]{1,0:T(8,128)(2,1)}, u32[]{:S(2)}, u32[]{:S(2)}) %collective-permute-start.1) | collective-permute-done | bytes 2457632 | tf_op jit(solution)/shard_map/ppermute | solution.py:60
  99.7 84.1 %collective-permute-done.2 = bf16[480,2560]{1,0:T(8,128)(2,1)S(1)} collective-permute-done((bf16[480,2560]{1,0:T(8,128)(2,1)}, bf16[480,2560]{1,0:T(8,128)(2,1)S(1)}, u32[]{:S(2)}, u32[]{:S(2)}) %collective-permute-start.2) | collective-permute-done | bytes 2457632 | tf_op jit(solution)/shard_map/ppermute | solution.py:60
  183.8 1.5 copy-done.3
  185.3 83.9 %collective-permute-done.3 = bf16[480,2560]{1,0:T(8,128)(2,1)S(1)} collective-permute-done((bf16[480,2560]{1,0:T(8,128)(2,1)S(1)}, bf16[480,2560]{1,0:T(8,128)(2,1)S(1)}, u32[]{:S(2)}, u32[]{:S(2)}) %collective-permute-start.3) | collective-permute-done | bytes 2457632 | tf_op jit(solution)/shard_map/ppermute | solution.py:60
  269.2 1.4 copy-done.4
  270.6 36.4 %collective-permute-done.4 = bf16[480,2560]{1,0:T(8,128)(2,1)S(1)} collective-permute-done((bf16[480,2560]{1,0:T(8,128)(2,1)S(1)}, bf16[480,2560]{1,0:T(8,128)(2,1)S(1)}, u32[]{:S(2)}, u32[]{:S(2)}) %collective-permute-start.4) | collective-permute-done | bytes 2457632 | tf_op jit(solution)/shard_map/ppermute | solution.py:60
  307.1 1.5 copy-done.5
  308.6 31.2 %collective-permute-done.5 = bf16[480,2560]{1,0:T(8,128)(2,1)} collective-permute-done((bf16[480,2560]{1,0:T(8,128)(2,1)S(1)}, bf16[480,2560]{1,0:T(8,128)(2,1)}, u32[]{:S(2)}, u32[]{:S(2)}) %collective-permute-start.5) | collective-permute-done | bytes 2457632 | tf_op jit(solution)/shard_map/ppermute | solution.py:60
  340.4 1.3 dynamic-slice
  341.8 0.8 dynamic-update-slice
  342.6 13.5 %all-reduce = s32[8]{0:T(128)S(1)} all-reduce(s32[8]{0:T(128)S(1)} %dynamic-update-slice), channel_id=1, replica_groups=mesh['cfg'=2,'seq'=8,'tp'=2] {'seq'}, use_global_device_ids=true, to_apply=%add | all-reduce | flops 8 | bytes 64
  356.1 4.4 copy.58
  360.5 2.9 copy.52
  364.1 4.4 copy.53
  368.5 4.4 copy.56
  373.0 0.1 select_reduce_fusion
  373.1 12.0 %fusion.6 = (f32[20,480]{1,0:T(8,128)S(1)}, f32[20,480,512]{2,1,0:T(8,128)}) fusion(pred[512]{0:T(512)(128)(4,1)S(1)} %iota_compare_fusion.2, bf16[480,20,128]{0,2,1:T(8,128)(2,1)S(1)} %bitcast.100, bf16[512,20,128]{0,2,1:T(8,128)(2,1)} %bitcast.105), kind=kOutput, calls=%fused_computation.10 | convolution fusion | flops 1273027200 | bytes 24778752 | tf_op jit(solution)/shard_map/qhd,khd->hqk/dot_general | solution.py:28
  385.1 4.4 copy.66
  389.5 4.4 copy.65
  393.8 4.4 copy.64
  398.2 4.4 copy.63
  402.6 4.4 copy.62
  407.0 4.4 copy.61
  411.3 4.3 copy.60
  415.7 60.8 %concatenate.6 = bf16[7680,2560]{0,1:T(8,128)(2,1)} concatenate(bf16[480,2560]{0,1:T(8,128)(2,1)} %copy.60, bf16[480,2560]{0,1:T(8,128)(2,1)} %copy.61, bf16[480,2560]{0,1:T(8,128)(2,1)} %copy.62, bf16[480,2560]{0,1:T(8,128)(2,1)} %copy.63, bf16[480,2560]{0,1:T(8,128)(2,1)} %copy.64, bf16[480,2560]{0,1:T(8,128)(2,1)} %copy.65, bf16[480,2560]{0,1:T(8,128)(2,1)} %copy.66, ...), dimensions={0} | concatenate | bytes 78643200 | tf_op jit(solution)/shard_map/jit(_roll_dynamic)/concatenate | solution.py:61
  476.4 19.2 %constant_dynamic-slice_fusion = bf16[3840,2560]{0,1:T(8,128)(2,1)} fusion(bf16[7680,2560]{0,1:T(8,128)(2,1)} %concatenate.6, s32[]{:T(128)S(6)} %select_n.75), kind=kLoop, calls=%fused_computation.78 | loop fusion | bytes 39321604 | tf_op jit(solution)/shard_map/jit(_roll_dynamic)/dynamic_slice | solution.py:61
  495.7 57.2 %bitcast_reduce_fusion = (f32[20,480]{1,0:T(8,128)S(1)}, f32[20,3840,480]{1,2,0:T(8,128)}) fusion(pred[3840]{0:T(1024)(128)(4,1)S(1)} %fusion.37, bf16[3840,20,128]{0,2,1:T(8,128)(2,1)} %bitcast.99, bf16[480,20,128]{0,2,1:T(8,128)(2,1)S(1)} %bitcast.101), kind=kOutput, calls=%fused_computation.1 | convolution fusion | flops 9547766784 | bytes 169616640 | tf_op jit(solution)/shard_map/qhd,khd->hqk/dot_general | solution.py:28
  552.9 9.8 %fusion.7 = f32[20,480]{1,0:T(8,128)S(1)} fusion(f32[20,480,512]{2,1,0:T(8,128)} %get-tuple-element.19, f32[20,480]{1,0:T(8,128)S(1)} %get-tuple-element.13, pred[512]{0:T(512)(128)(4,1)S(1)} %iota_compare_fusion.2), kind=kLoop, calls=%fused_computation.11 | loop fusion | flops 19651200 | bytes 19738112 | tf_op jit(solution)/shard_map/reduce_sum | solution.py:35
  562.7 45.0 %fusion.1 = f32[20,480]{1,0:T(8,128)S(1)} fusion(f32[20,3840,480]{1,2,0:T(8,128)} %get-tuple-element.17, f32[20,480]{1,0:T(8,128)S(1)} %get-tuple-element.12, pred[3840]{0:T(1024)(128)(4,1)S(1)} %fusion.37), kind=kLoop, calls=%fused_computation.4 | loop fusion | flops 147446400 | bytes 147536640 | tf_op jit(solution)/shard_map/reduce_sum | solution.py:35
  607.7 10.3 %fusion.9 = f32[20,480,128]{2,1,0:T(8,128)} fusion(bf16[512,20,128]{0,2,1:T(8,128)(2,1)S(1)} %bitcast.111, f32[20,480,512]{2,1,0:T(8,128)} %get-tuple-element.19, f32[20,480]{1,0:T(8,128)S(1)} %get-tuple-element.13, pred[512]{0:T(512)(128)(4,1)S(1)} %iota_compare_fusion.2), kind=kOutput, calls=%fused_computation.13 | convolution fusion | flops 1277952000 | bytes 27236352 | tf_op jit(solution)/shard_map/hqk,khd->hqd/dot_general | solution.py:36
  618.0 24.1 %copy.76 = bf16[1,3840,2560]{1,2,0:T(8,128)(2,1)} copy(bf16[1,3840,2560]{2,1,0:T(8,128)(2,1)} %all-gather.5.cloned.1.call-done) | data formatting | bytes 39321600 | tf_op jit(solution)/shard_map/all_gather | solution.py:64
  642.1 55.6 %fusion.17 = bf16[480,20,128]{2,0,1:T(8,128)(2,1)} fusion(f32[20,480,128]{2,1,0:T(8,128)} %fusion.9, f32[480,20]{0,1:T(8,128)S(1)} %get-tuple-element.9, f32[480,20]{0,1:T(8,128)S(1)} %get-tuple-element.10, f32[480,20]{0,1:T(8,128)S(1)} %get-tuple-element.11, bf16[3840,20,128]{0,2,1:T(8,128)(2,1)} %bitcast.104, f32[20,3840,480]{1,2,0:T(8,128)} %get-tuple-element.17, ...), kind=kOutput, calls=%fused_computation.22 | convolution fusion | flops 9590784000 | bytes 174647040 | tf_op jit(solution)/shard_map/hqk,khd->hqd/dot_general | solution.py:36
  697.7 2.9 copy.78
  700.6 19.7 %fusion.15 = bf16[5120,480]{0,1:T(8,128)(2,1)} fusion(bf16[480,2560]{0,1:T(8,128)(2,1)S(1)} %bitcast.112, bf16[2560,5120]{1,0:T(8,128)(2,1)} %param.15), kind=kOutput, calls=%fused_computation.19 | convolution fusion | flops 12585369600 | bytes 33587200 | tf_op jit(solution)/shard_map/dot_general | solution.py:76
  720.4 0.0 all-gather.7.cloned.1.call-start
  720.4 81.9 %reduce-scatter.2.cloned.1.call-done = bf16[2560,480]{0,1:T(8,128)(2,1)} async-done(((bf16[5120,480]{0,1:T(8,128)(2,1)}), bf16[2560,480]{0,1:T(8,128)(2,1)}) %reduce-scatter.2.cloned.1.call-update) | async-done | bytes 2457616 | tf_op jit(solution)/shard_map/reduce_scatter | solution.py:75
  802.4 0.7 reduce_sum.49
  803.7 65.1 %all-gather.7.cloned.1.call-done = bf16[960,2560]{1,0:T(8,128)(2,1)} async-done(((bf16[480,2560]{1,0:T(8,128)(2,1)}), bf16[960,2560]{1,0:T(8,128)(2,1)}) %all-gather.7.cloned.1.call-update) | async-done | bytes 4915216 | tf_op jit(solution)/shard_map/all_gather | solution.py:88
  868.8 1.7 convolution_reduce_fusion
  870.5 2.4 fusion.28
  873.0 2.9 fusion.29
  875.9 1.4 fusion.30
  877.3 28.4 %all-reduce.1 = (f32[1280]{0:T(1024)S(1)}, f32[1280]{0:T(1024)S(1)}, f32[1280]{0:T(1024)S(1)}, f32[1280]{0:T(1024)S(1)}) all-reduce(f32[1280]{0:T(1024)S(1)} %fusion.30, f32[1280]{0:T(1024)S(1)} %convolution_reduce_fusion, f32[1280]{0:T(1024)S(1)} %fusion.28, f32[1280]{0:T(1024)S(1)} %fusion.29), channel_id=1, replica_groups=mesh['cfg'=2,'seq'=8,'tp'=2] {'seq'}, use_global_device_ids=true, to_apply=%region_10.11 | all-reduce | flops 5120 | bytes 40960 | tf_op jit(solution)/shard_map/psum | solution.py:100
  905.7 3.4 add_convert_fusion
  (33 shorter events, 0.2 us)
Async XLA Ops:
  6.5 611.5 %all-gather.5.cloned.1.call-start = ((), (), s32[]{:S(2)}) async-start(), calls=%async_computation.2 | async-start | bytes 22118400 | tf_op jit(solution)/shard_map/all_gather | solution.py:64
  6.5 32.3 %collective-permute-start = (bf16[480,2560]{1,0:T(8,128)(2,1)}, bf16[480,2560]{1,0:T(8,128)(2,1)S(1)}, u32[]{:S(2)}, u32[]{:S(2)}) collective-permute-start(bf16[480,2560]{1,0:T(8,128)(2,1)} %bitcast.114), channel_id=1, source_target_pairs={{0,2},{2,4},{4,6},{6,8},{8,10},{10,12},{12,14},{14,0},{1,3},{3,5},... | collective-permute-start | bytes 7372808 | tf_op jit(solution)/shard_map/ppermute | solution.py:60
  38.8 321.6 %copy-start.2 = (bf16[480,2560]{1,0:T(8,128)(2,1)}, bf16[480,2560]{1,0:T(8,128)(2,1)S(1)}, u32[]{:S(2)}) copy-start(bf16[480,2560]{1,0:T(8,128)(2,1)S(1)} %collective-permute-done) | copy-start | bytes 7372804
  38.8 60.9 %collective-permute-start.1 = (bf16[480,2560]{1,0:T(8,128)(2,1)S(1)}, bf16[480,2560]{1,0:T(8,128)(2,1)}, u32[]{:S(2)}, u32[]{:S(2)}) collective-permute-start(bf16[480,2560]{1,0:T(8,128)(2,1)S(1)} %collective-permute-done), channel_id=1, source_target_pairs={{0,2},{2,4},{4,6},{6,8},{8,10},{10,12},{12,14},{14,0},{1,3},{3,5},... | collective-permute-start | bytes 7372808 | tf_op jit(solution)/shard_map/ppermute | solution.py:60
  38.9 763.5 %reduce-scatter.2.cloned.1.call-start = ((), (), s32[]{:S(2)}) async-start(), calls=%async_computation.1 | async-start | bytes 7372800 | tf_op jit(solution)/shard_map/reduce_scatter | solution.py:75
  99.7 84.1 %collective-permute-start.2 = (bf16[480,2560]{1,0:T(8,128)(2,1)}, bf16[480,2560]{1,0:T(8,128)(2,1)S(1)}, u32[]{:S(2)}, u32[]{:S(2)}) collective-permute-start(bf16[480,2560]{1,0:T(8,128)(2,1)} %collective-permute-done.1), channel_id=1, source_target_pairs={{0,2},{2,4},{4,6},{6,8},{8,10},{10,12},{12,14},{14,0},{1,3},{3,5},... | collective-permute-start | bytes 7372808 | tf_op jit(solution)/shard_map/ppermute | solution.py:60
  183.8 1.5 copy-start.3
  185.3 83.9 %collective-permute-start.3 = (bf16[480,2560]{1,0:T(8,128)(2,1)S(1)}, bf16[480,2560]{1,0:T(8,128)(2,1)S(1)}, u32[]{:S(2)}, u32[]{:S(2)}) collective-permute-start(bf16[480,2560]{1,0:T(8,128)(2,1)S(1)} %collective-permute-done.2), channel_id=1, source_target_pairs={{0,2},{2,4},{4,6},{6,8},{8,10},{10,12},{12,14},{14,0},{1,3},{3,5},... | collective-permute-start | bytes 7372808 | tf_op jit(solution)/shard_map/ppermute | solution.py:60
  269.2 1.4 copy-start.4
  270.6 36.4 %collective-permute-start.4 = (bf16[480,2560]{1,0:T(8,128)(2,1)S(1)}, bf16[480,2560]{1,0:T(8,128)(2,1)S(1)}, u32[]{:S(2)}, u32[]{:S(2)}) collective-permute-start(bf16[480,2560]{1,0:T(8,128)(2,1)S(1)} %collective-permute-done.3), channel_id=1, source_target_pairs={{0,2},{2,4},{4,6},{6,8},{8,10},{10,12},{12,14},{14,0},{1,3},{3,5},... | collective-permute-start | bytes 7372808 | tf_op jit(solution)/shard_map/ppermute | solution.py:60
  307.1 1.5 copy-start.5
  308.6 31.2 %collective-permute-start.5 = (bf16[480,2560]{1,0:T(8,128)(2,1)S(1)}, bf16[480,2560]{1,0:T(8,128)(2,1)}, u32[]{:S(2)}, u32[]{:S(2)}) collective-permute-start(bf16[480,2560]{1,0:T(8,128)(2,1)S(1)} %collective-permute-done.4), channel_id=1, source_target_pairs={{0,2},{2,4},{4,6},{6,8},{8,10},{10,12},{12,14},{14,0},{1,3},{3,5},... | collective-permute-start | bytes 7372808 | tf_op jit(solution)/shard_map/ppermute | solution.py:60
  339.8 71.5 %collective-permute-start.6 = (bf16[480,2560]{1,0:T(8,128)(2,1)}, bf16[480,2560]{1,0:T(8,128)(2,1)}, u32[]{:S(2)}, u32[]{:S(2)}) collective-permute-start(bf16[480,2560]{1,0:T(8,128)(2,1)} %collective-permute-done.5), channel_id=1, source_target_pairs={{0,2},{2,4},{4,6},{6,8},{8,10},{10,12},{12,14},{14,0},{1,3},{3,5},... | collective-permute-start | bytes 7372808 | tf_op jit(solution)/shard_map/ppermute | solution.py:60
  356.1 16.9 %copy-start.6 = (s32[8]{0:T(128)}, s32[8]{0:T(128)S(1)}, u32[]{:S(2)}) copy-start(s32[8]{0:T(128)S(1)} %all-reduce) | copy-start | bytes 100
  562.7 45.0 %copy-start.1 = (bf16[1,512,2560]{1,2,0:T(8,128)(2,1)S(1)}, bf16[1,512,2560]{1,2,0:T(8,128)(2,1)}, u32[]{:S(2)}) copy-start(bf16[1,512,2560]{1,2,0:T(8,128)(2,1)} %copy.56) | copy-start | bytes 7864324
  720.4 82.0 %copy-start.7 = (s32[8]{0:T(128)S(1)}, s32[8]{0:T(128)}, u32[]{:S(2)}) copy-start(s32[8]{0:T(128)} %copy-done.6) | copy-start | bytes 100
  720.4 148.4 %all-gather.7.cloned.1.call-start = ((), (), s32[]{:S(2)}) async-start(), calls=%async_computation.3 | async-start | bytes 7372800 | tf_op jit(solution)/shard_map/all_gather | solution.py:88
  868.8 7.1 copy-start
Sparse Core Ops, SparseCore 0:
  39.0 246.1 all-gather.4
  720.5 81.8 reduce-scatter.1
  803.9 64.8 all-gather.6
